TPU v7x, 32 devices: a whole 2x2x4 slice. The times are simulated.
32 devices in a mesh: unit: 4 (over z), bank: 4 (over x, core), zero: 2 (over y).
Axes of the slice: x: 2, y: 2, z: 4, core: 2. Of those that a mesh axis runs over, the one named last changes fastest.
Arguments:
- train_down: float32 [256, 1024, 2048], P(('unit', 'bank'), None, 'zero'), parts along dimension 0, may hold values from -0.25 to 0.25
- router_weight: float32 [8192, 64], P(('unit', 'zero'), 'bank'), parts along dimension 0, may hold values from -0.125 to 0.125
- router_gain: float32 [8192], P(('unit', 'zero')), parts along dimension 0, may hold values from 0.25 to 1.75
Outputs:
- ready_down: bfloat16 [256, 1024, 2048], P(('unit', 'bank'), 'zero'), parts along dimension 0
- scale_down: float32 [256, 1024], P(('unit', 'bank'), 'zero'), parts along dimension 0
- serve_router: bfloat16 [8192, 64], P('unit'), parts along dimension 0
There are 4 independent parts, one for each index of `unit`. A program takes and returns all parts, laid end to end along the dimension named above; each array names one. Nothing has to cross between parts.
All inputs are finite; a program needn't handle non-finite values.
Results may differ from a plain program's by a relative error of at most 0.001.
Values may be sent and summed in bfloat16 or wider, within the bound.
A program may use at most 256 MiB of HBM per device.

v0:
```python
import jax
import jax.numpy as jnp
from jax import lax
from jax.sharding import PartitionSpec as P


def per_device(train_down, router_weight, router_gain):
    scale_down = lax.pmax(jnp.max(jnp.abs(train_down), axis=2), "zero")
    narrow_down = (train_down / jnp.expand_dims(scale_down, 2)).astype(jnp.bfloat16)
    ready_down = lax.all_to_all(narrow_down, "zero", split_axis=1, concat_axis=2, tiled=True)
    scale_down = lax.dynamic_slice_in_dim(
        scale_down, lax.axis_index("zero") * ready_down.shape[1], ready_down.shape[1], axis=1
    )
    part_router = (router_weight * router_gain[:, None]).astype(jnp.bfloat16)
    row_router = lax.all_gather(part_router, "zero", axis=0, tiled=True)
    serve_router = lax.all_gather(row_router, "bank", axis=1, tiled=True)
    return (ready_down, scale_down, serve_router)


def solution(mesh):
    in_specs = (P(("unit", "bank"), None, "zero"), P(("unit", "zero"), "bank"), P(("unit", "zero")))
    out_specs = (P(("unit", "bank"), "zero", None), P(("unit", "bank"), "zero"), P("unit", None))
    return jax.shard_map(
        per_device, mesh=mesh, in_specs=in_specs, out_specs=out_specs, check_vma=False
    )
```

profile of v0, /device:TPU:0, one launch (start us, length us, event | category | flops | bytes accessed | tf_op | source)
XLA Modules:
  0.0 617.8 jit_solution(3817814109771987231)
XLA Ops:
  7.2 0.0 all-reduce.2.cloned.1.call-start
  7.2 21.4 %abs_reduce_fusion = f32[16,1024]{1,0:T(8,128)} fusion(f32[16,1024,1024]{2,1,0:T(8,128)} %param.3), kind=kLoop, calls=%fused_computation.2 | loop fusion | flops 33538048 | bytes 67174400 | tf_op jit(solution)/shard_map/reduce_max | solution.py:8
  28.6 0.0 all-reduce.2.cloned.1.call-update
  28.6 23.8 %all-reduce.2.cloned.1.call-done = f32[16,1024]{1,0:T(8,128)} async-done(((f32[16,1024]{1,0:T(8,128)}), f32[16,1024]{1,0:T(8,128)}) %all-reduce.2.cloned.1.call-update) | async-done | bytes 65552 | tf_op jit(solution)/shard_map/pmax | solution.py:8
  52.5 1.0 copy.7
  53.5 0.0 copy-start.1
  53.5 0.0 copy-start.2
  53.6 0.0 copy-start
  53.6 60.1 %fusion = bf16[16,1024,1024]{2,0,1:T(8,128)(2,1)} fusion(f32[16,1024,1024]{2,1,0:T(8,128)} %param.3, f32[16,1024]{0,1:T(8,128)S(1)} %copy.7), kind=kLoop, calls=%fused_computation.1 | loop fusion | flops 33554432 | bytes 100728832 | tf_op jit(solution)/shard_map/convert_element_type | solution.py:9
  113.7 13.0 %all-to-all-start = ((bf16[16,1024,1024]{2,0,1:T(8,128)(2,1)}), bf16[16,1024,1024]{2,0,1:T(8,128)(2,1)}, u32[]{:S(2)}, u32[]{:S(2)}) async-start(bf16[16,1024,1024]{2,0,1:T(8,128)(2,1)} %fusion), calls=%async_computation | async-start | bytes 67108864 | tf_op jit(solution)/shard_map/all_to_all | solution.py:10
  126.7 0.0 copy-done.1
  126.7 0.0 copy-done.2
  126.7 362.4 %all_gather.6 = bf16[2048,16]{0,1:T(8,128)(2,1)S(1)} all-gather(bf16[1024,16]{0,1:T(8,128)(2,1)S(1)} %multiply_convert_fusion), channel_id=1, replica_groups=mesh['unit'=4,'bank'=4,'zero'=2] {'zero'}, dimensions={0}, use_global_device_ids=true | all-gather | bytes 98304 | tf_op jit(solution)/shard_map/all_gather | solution.py:15
  489.1 5.8 all_gather.7
  494.8 0.0 copy-done
  494.8 0.6 constant_dynamic-slice_fusion
  495.5 0.0 all-to-all-done
  495.5 60.5 %copy.9 = bf16[16,512,2,1024]{3,2,1,0:T(2,128)(2,1)} copy(bf16[16,512,2,1024]{3,0,1,2:T(8,128)(2,1)} %bitcast.1) | data formatting | bytes 67108864 | tf_op jit(solution)/shard_map/all_to_all | solution.py:10
  556.0 54.2 %all_to_all.16 = bf16[16,512,2048]{2,1,0:T(8,128)(2,1)} reshape(bf16[16,512,2,1024]{3,2,1,0:T(2,128)(2,1)} %copy.9) | data formatting | bytes 67108864 | tf_op jit(solution)/shard_map/all_to_all | solution.py:10
  610.2 0.7 copy.15
  (1 shorter events, 0.0 us)
Async XLA Ops:
  7.2 45.3 %all-reduce.2.cloned.1.call-start = ((), (), s32[]{:S(2)}) async-start(), calls=%async_computation.1 | async-start | bytes 131072 | tf_op jit(solution)/shard_map/pmax | solution.py:8
  53.5 73.1 %copy-start.1 = (f32[1024,16]{0,1:T(8,128)S(1)}, f32[1024,16]{0,1:T(8,128)}, u32[]{:S(2)}) copy-start(f32[1024,16]{0,1:T(8,128)} %param.4) | copy-start | bytes 196612
  53.5 73.1 %copy-start.2 = (f32[1024]{0:T(1024)S(1)}, f32[1024]{0:T(1024)}, u32[]{:S(2)}) copy-start(f32[1024]{0:T(1024)} %param.5) | copy-start | bytes 12292
  53.6 441.3 %copy-start = (f32[16,1024]{1,0:T(8,128)S(1)}, f32[16,1024]{1,0:T(8,128)}, u32[]{:S(2)}) copy-start(f32[16,1024]{1,0:T(8,128)} %all-reduce.2.cloned.1.call-done) | copy-start | bytes 196612
  113.7 381.8 %all-to-all-start = ((bf16[16,1024,1024]{2,0,1:T(8,128)(2,1)}), bf16[16,1024,1024]{2,0,1:T(8,128)(2,1)}, u32[]{:S(2)}, u32[]{:S(2)}) async-start(bf16[16,1024,1024]{2,0,1:T(8,128)(2,1)} %fusion), calls=%async_computation | async-start | bytes 67108864 | tf_op jit(solution)/shard_map/all_to_all | solution.py:10
Sparse Core Ops, SparseCore 0:
  28.8 23.6 all-reduce.1
where the time goes:
time: 619 us; the launch traced here: 618 us
  blocking collectives  368 us (59%)
  local copies, waits for them, and re-layouts  117 us (19%)
  other arithmetic  81.6 us (13%)
  waiting for transfers between devices  23.9 us (4%)
  between operations  14.1 us (2%)
  starting transfers between devices  13 us (2%)
    all_gather x1, blocking collectives, per_device(): row_router = lax.all_gather(part_router, 'zero', axis=0, tiled=True)  362 us
    all_to_all x2, local copies, waits for them, and re-layouts, per_device(): lax.all_to_all(narrow_down, 'zero', split_axis=1, concat_axis=2, tiled=True)  115 us
    convert_element_type x1, other arithmetic, per_device(): (train_down / jnp.expand_dims(scale_down, 2)).astype(jnp.bfloat16)  60.1 us
    pmax x1, waiting for transfers between devices, per_device(): scale_down = lax.pmax(jnp.max(jnp.abs(train_down), axis=2), 'zero')  23.8 us
    reduce_max x1, other arithmetic, per_device(): scale_down = lax.pmax(jnp.max(jnp.abs(train_down), axis=2), 'zero')  21.4 us
    all_to_all x1, starting transfers between devices, per_device(): lax.all_to_all(narrow_down, 'zero', split_axis=1, concat_axis=2, tiled=True)  13 us
  transfers between devices with their start and end apart: 2, of which 1 were waited for; matrix products, arithmetic and copies ran while one was open for 0% of the time, Pallas kernels for 0%

commit v1 on v0

--- a/solution.py
+++ b/solution.py
@@ -7,7 +7,13 @@
 def per_device(train_down, router_weight, router_gain):
     scale_down = lax.pmax(jnp.max(jnp.abs(train_down), axis=2), "zero")
     narrow_down = (train_down / jnp.expand_dims(scale_down, 2)).astype(jnp.bfloat16)
-    ready_down = lax.all_to_all(narrow_down, "zero", split_axis=1, concat_axis=2, tiled=True)
+    build_values = lambda mine: jnp.concatenate(
+        lax.all_to_all(
+            jnp.stack(jnp.split(mine, lax.axis_size("zero"), axis=1), axis=0), "zero", 0, 0
+        ),
+        axis=2,
+    )
+    ready_down = build_values(narrow_down)
     scale_down = lax.dynamic_slice_in_dim(
         scale_down, lax.axis_index("zero") * ready_down.shape[1], ready_down.shape[1], axis=1
     )

time: 619 us -> 544 us (0.88)
  local copies, waits for them, and re-layouts: 117 us -> 47.7 us
    all_to_all x2 -> x0, local copies, waits for them, and re-layouts: 115 us -> none  [per_device(): lax.all_to_all(narrow_down, 'zero', split_axis=1, concat_axis=2, tiled=True)]
    convert_element_type x1, other arithmetic: 60.1 us -> 32.9 us  [per_device(): (train_down / jnp.expand_dims(scale_down, 2)).astype(jnp.bfloat16)]
    reshape x0 -> x1, local copies, waits for them, and re-layouts: none -> 23.3 us  [per_device(): jnp.concatenate(lax.all_to_all(jnp.stack(jnp.split(mine, lax.axis_size('z...]
    another operation x0 -> x1, local copies, waits for them, and re-layouts: none -> 23.1 us  [per_device(): jnp.stack(jnp.split(mine, lax.axis_size('zero'), axis=1), axis=0)]
    another operation x0 -> x1, other arithmetic: none -> 23 us  [per_device(): jnp.stack(jnp.split(mine, lax.axis_size('zero'), axis=1), axis=0)]
where the time goes in v1:
time: 544 us
  blocking collectives  368 us (68%)
  other arithmetic  77.3 us (14%)
  local copies, waits for them, and re-layouts  47.7 us (9%)
  waiting for transfers between devices  23.9 us (4%)
  between operations  14.1 us (3%)
  starting transfers between devices  13.1 us (2%)
    all_gather x1, blocking collectives, per_device(): row_router = lax.all_gather(part_router, 'zero', axis=0, tiled=True)  362 us
    convert_element_type x1, other arithmetic, per_device(): (train_down / jnp.expand_dims(scale_down, 2)).astype(jnp.bfloat16)  32.9 us
    pmax x1, waiting for transfers between devices, per_device(): scale_down = lax.pmax(jnp.max(jnp.abs(train_down), axis=2), 'zero')  23.8 us
    reshape x1, local copies, waits for them, and re-layouts, per_device(): jnp.concatenate(lax.all_to_all(jnp.stack(jnp.split(mine, lax.axis_size('z...  23.3 us
    another operation x1, local copies, waits for them, and re-layouts, per_device(): jnp.stack(jnp.split(mine, lax.axis_size('zero'), axis=1), axis=0)  23.1 us
    another operation x1, other arithmetic, per_device(): jnp.stack(jnp.split(mine, lax.axis_size('zero'), axis=1), axis=0)  23 us
    reduce_max x1, other arithmetic, per_device(): scale_down = lax.pmax(jnp.max(jnp.abs(train_down), axis=2), 'zero')  21.4 us
    all_to_all x1, starting transfers between devices, per_device(): lax.all_to_all(jnp.stack(jnp.split(mine, lax.axis_size('zero'), axis=1),...  13.1 us
  transfers between devices with their start and end apart: 2, of which 1 were waited for; matrix products, arithmetic and copies ran while one was open for 0% of the time, Pallas kernels for 0%

profile of v1, /device:TPU:0, one launch (start us, length us, event | category | flops | bytes accessed | tf_op | source)
XLA Modules:
  0.0 544.2 jit_solution(9817326848428863188)
XLA Ops:
  7.2 0.0 all-reduce.2.cloned.1.call-start
  7.2 21.4 %abs_reduce_fusion = f32[16,1024]{1,0:T(8,128)} fusion(f32[16,1024,1024]{2,1,0:T(8,128)} %param.3), kind=kLoop, calls=%fused_computation.1 | loop fusion | flops 33538048 | bytes 67174400 | tf_op jit(solution)/shard_map/reduce_max | solution.py:8
  28.6 0.0 all-reduce.2.cloned.1.call-update
  28.6 23.8 %all-reduce.2.cloned.1.call-done = f32[16,1024]{1,0:T(8,128)} async-done(((f32[16,1024]{1,0:T(8,128)}), f32[16,1024]{1,0:T(8,128)}) %all-reduce.2.cloned.1.call-update) | async-done | bytes 65552 | tf_op jit(solution)/shard_map/pmax | solution.py:8
  52.5 32.9 %divide_convert_fusion = bf16[16,1024,1024]{2,1,0:T(8,128)(2,1)} fusion(f32[16,1024,1024]{2,1,0:T(8,128)} %param.3, f32[16,1024]{1,0:T(8,128)} %all-reduce.2.cloned.1.call-done), kind=kLoop, calls=%fused_computation | loop fusion | flops 33554432 | bytes 100728832 | tf_op jit(solution)/shard_map/convert_element_type | solution.py:9
  85.4 23.1 %slice_bitcast_fusion.1 = (bf16[1,16,512,1024]{3,2,1,0:T(8,128)(2,1)}, bf16[1,16,512,1024]{3,2,1,0:T(8,128)(2,1)}) fusion(bf16[16,1024,1024]{2,1,0:T(8,128)(2,1)} %divide_convert_fusion), kind=kLoop, calls=%fused_computation.4 | loop fusion | bytes 67108864 | tf_op jit(solution)/shard_map/stack | solution.py:12
  108.5 23.0 %pad_maximum_fusion = bf16[2,16,512,1024]{3,2,1,0:T(8,128)(2,1)} fusion(bf16[1,16,512,1024]{3,2,1,0:T(8,128)(2,1)} %get-tuple-element.4, bf16[1,16,512,1024]{3,2,1,0:T(8,128)(2,1)} %get-tuple-element.3), kind=kLoop, calls=%fused_computation.2 | loop fusion | flops 16777216 | bytes 67108864 | tf_op jit(solution)/shard_map/stack | solution.py:12
  131.4 0.0 copy-start.1
  131.5 0.0 copy-start.2
  131.5 0.0 copy-start
  131.5 13.1 %all-to-all-start = ((bf16[2,16,512,1024]{3,2,1,0:T(8,128)(2,1)}), bf16[2,16,512,1024]{3,2,1,0:T(8,128)(2,1)}, u32[]{:S(2)}, u32[]{:S(2)}) async-start(bf16[2,16,512,1024]{3,2,1,0:T(8,128)(2,1)} %pad_maximum_fusion), calls=%async_computation | async-start | bytes 67108864 | tf_op jit(solution)/shard_map/all_to_all | solution.py:11
  144.6 0.0 copy-done.1
  144.6 0.0 copy-done.2
  144.6 362.4 %all_gather.6 = bf16[2048,16]{0,1:T(8,128)(2,1)S(1)} all-gather(bf16[1024,16]{0,1:T(8,128)(2,1)S(1)} %multiply_convert_fusion), channel_id=1, replica_groups=mesh['unit'=4,'bank'=4,'zero'=2] {'zero'}, dimensions={0}, use_global_device_ids=true | all-gather | bytes 98304 | tf_op jit(solution)/shard_map/all_gather | solution.py:21
  507.0 5.8 %all_gather.7 = bf16[2048,64]{0,1:T(8,128)(2,1)S(1)} all-gather(bf16[2048,16]{0,1:T(8,128)(2,1)S(1)} %all_gather.6), channel_id=1, replica_groups=mesh['unit'=4,'bank'=4,'zero'=2] {'bank'}, dimensions={1}, use_global_device_ids=true | all-gather | bytes 327680 | tf_op jit(solution)/shard_map/all_gather | solution.py:22
  512.8 0.0 copy-done
  512.8 0.6 constant_dynamic-slice_fusion
  513.4 0.0 all-to-all-done
  513.4 23.3 %copy.7 = bf16[2,16,64,8,1024]{4,3,0,2,1:T(8,128)(2,1)} copy(bf16[2,16,64,8,1024]{4,3,2,1,0:T(8,128)(2,1)} %bitcast.3) | data formatting | bytes 67108864 | tf_op jit(solution)/shard_map/reshape | solution.py:10
  536.7 0.7 copy.10
  (1 shorter events, 0.0 us)
Async XLA Ops:
  7.2 45.3 %all-reduce.2.cloned.1.call-start = ((), (), s32[]{:S(2)}) async-start(), calls=%async_computation.1 | async-start | bytes 131072 | tf_op jit(solution)/shard_map/pmax | solution.py:8
  131.4 13.2 %copy-start.1 = (f32[1024,16]{0,1:T(8,128)S(1)}, f32[1024,16]{0,1:T(8,128)}, u32[]{:S(2)}) copy-start(f32[1024,16]{0,1:T(8,128)} %param.4) | copy-start | bytes 196612
  131.5 13.2 %copy-start.2 = (f32[1024]{0:T(1024)S(1)}, f32[1024]{0:T(1024)}, u32[]{:S(2)}) copy-start(f32[1024]{0:T(1024)} %param.5) | copy-start | bytes 12292
  131.5 381.3 %copy-start = (f32[16,1024]{1,0:T(8,128)S(1)}, f32[16,1024]{1,0:T(8,128)}, u32[]{:S(2)}) copy-start(f32[16,1024]{1,0:T(8,128)} %all-reduce.2.cloned.1.call-done) | copy-start | bytes 196612
  131.5 381.9 %all-to-all-start = ((bf16[2,16,512,1024]{3,2,1,0:T(8,128)(2,1)}), bf16[2,16,512,1024]{3,2,1,0:T(8,128)(2,1)}, u32[]{:S(2)}, u32[]{:S(2)}) async-start(bf16[2,16,512,1024]{3,2,1,0:T(8,128)(2,1)} %pad_maximum_fusion), calls=%async_computation | async-start | bytes 67108864 | tf_op jit(solution)/shard_map/all_to_all | solution.py:11
Sparse Core Ops, SparseCore 0:
  28.8 23.6 all-reduce.1
